TPU v7x, 16 devices: a whole 2x2x2 slice. The times are simulated.
16 devices in a mesh: col: 2 (over z), row: 8 (over y, x, core).
Axes of the slice: x: 2, y: 2, z: 2, core: 2. Of those that a mesh axis runs over, the one named last changes fastest.
Arguments:
- adjacency: bfloat16 [24576, 24576], P('row', 'col')
- pers_vec: float32 [24576, 64], P(('row', 'col'))
- restart_wt: float32 [16, 64], replicated
Outputs:
- output 1: float32 [24576, 64], P(('col', 'row'))
- output 2: float32 [24576, 64], P(('row', 'col'))
All inputs are finite; a program needn't handle non-finite values.
Results may differ from a plain program's by a relative error of at most 0.001.
Values are sent between devices in bfloat16 or wider.
A program may use at most 1 GiB of HBM per device.

v0:
```python
import jax
import jax.numpy as jnp
from jax import lax
from jax.sharding import PartitionSpec as P


def col_normalise(local_vals, n_total):
    sq_sum = lax.psum(jnp.sum(local_vals * local_vals, axis=0, keepdims=True), ("col", "row"))
    return local_vals * lax.rsqrt(sq_sum / n_total)


def solution(mesh):
    row_size = mesh.shape["row"]

    def device_fn(adj_tile, pers_piece, restart_wt):
        n_total = adj_tile.shape[0] * row_size
        hub_vec = pers_piece
        for sweep_idx in range(restart_wt.shape[0]):
            weight = restart_wt[sweep_idx]
            hub_block = lax.all_gather(hub_vec.astype(jnp.bfloat16), "col", axis=0, tiled=True)
            auth_part = lax.dot_general(adj_tile, hub_block, (((0,), (0,)), ((), ())), preferred_element_type=jnp.float32)
            auth_sum = lax.psum_scatter(auth_part, "row", scatter_dimension=0, tiled=True)
            auth_vec = col_normalise(auth_sum, n_total)
            auth_block = lax.all_gather(auth_vec.astype(jnp.bfloat16), "row", axis=0, tiled=True)
            hub_part = jnp.dot(adj_tile, auth_block, preferred_element_type=jnp.float32)
            hub_sum = lax.psum_scatter(hub_part, "col", scatter_dimension=0, tiled=True)
            hub_vec = (1.0 - weight) * col_normalise(hub_sum, n_total) + weight * pers_piece
        return auth_vec, hub_vec

    return jax.shard_map(device_fn, mesh=mesh, in_specs=(P("row", "col"), P(("row", "col"), None), P(None, None)), out_specs=(P(("col", "row"), None), P(("row", "col"), None)), check_vma=False)
```

profile of v0, /device:TPU:0, one launch (start us, length us, event | category | flops | bytes accessed | tf_op | source)
XLA Modules:
  0.0 3458.2 jit_solution(6704131071471461365)
XLA Ops:
  46.2 41.6 %reduce-scatter.33.cloned.1.call-done = f32[1536,64]{0,1:T(8,128)} async-done(((f32[12288,64]{0,1:T(8,128)}), f32[1536,64]{0,1:T(8,128)}) %reduce-scatter.33.cloned.1.call-update) | async-done | bytes 393232 | tf_op jit(solution)/shard_map/reduce_scatter | solution.py:22
  88.9 31.9 psum.224
  145.1 30.9 convolution_bitcast_fusion.30
  192.9 31.8 psum.225
  262.0 40.6 %reduce-scatter.37.cloned.1.call-done = f32[1536,64]{0,1:T(8,128)} async-done(((f32[12288,64]{0,1:T(8,128)}), f32[1536,64]{0,1:T(8,128)}) %reduce-scatter.37.cloned.1.call-update) | async-done | bytes 393232 | tf_op jit(solution)/shard_map/reduce_scatter | solution.py:22
  303.8 31.9 psum.226
  360.0 30.9 convolution_bitcast_fusion.29
  407.8 31.9 psum.227
  477.0 40.6 %reduce-scatter.41.cloned.1.call-done = f32[1536,64]{0,1:T(8,128)} async-done(((f32[12288,64]{0,1:T(8,128)}), f32[1536,64]{0,1:T(8,128)}) %reduce-scatter.41.cloned.1.call-update) | async-done | bytes 393232 | tf_op jit(solution)/shard_map/reduce_scatter | solution.py:22
  518.7 31.9 psum.228
  574.9 30.9 convolution_bitcast_fusion.28
  622.7 31.9 psum.229
  692.1 40.6 %reduce-scatter.45.cloned.1.call-done = f32[1536,64]{0,1:T(8,128)} async-done(((f32[12288,64]{0,1:T(8,128)}), f32[1536,64]{0,1:T(8,128)}) %reduce-scatter.45.cloned.1.call-update) | async-done | bytes 393232 | tf_op jit(solution)/shard_map/reduce_scatter | solution.py:22
  733.9 31.9 psum.230
  790.1 30.9 convolution_bitcast_fusion.27
  837.9 31.8 psum.231
  907.0 40.6 %reduce-scatter.49.cloned.1.call-done = f32[1536,64]{0,1:T(8,128)} async-done(((f32[12288,64]{0,1:T(8,128)}), f32[1536,64]{0,1:T(8,128)}) %reduce-scatter.49.cloned.1.call-update) | async-done | bytes 393232 | tf_op jit(solution)/shard_map/reduce_scatter | solution.py:22
  948.7 31.9 psum.232
  1004.9 30.9 convolution_bitcast_fusion.26
  1052.7 31.8 psum.233
  1121.9 40.6 %reduce-scatter.53.cloned.1.call-done = f32[1536,64]{0,1:T(8,128)} async-done(((f32[12288,64]{0,1:T(8,128)}), f32[1536,64]{0,1:T(8,128)}) %reduce-scatter.53.cloned.1.call-update) | async-done | bytes 393232 | tf_op jit(solution)/shard_map/reduce_scatter | solution.py:22
  1163.6 31.9 psum.234
  1219.8 30.9 convolution_bitcast_fusion.25
  1267.6 31.9 psum.235
  1336.8 40.6 %reduce-scatter.57.cloned.1.call-done = f32[1536,64]{0,1:T(8,128)} async-done(((f32[12288,64]{0,1:T(8,128)}), f32[1536,64]{0,1:T(8,128)}) %reduce-scatter.57.cloned.1.call-update) | async-done | bytes 393232 | tf_op jit(solution)/shard_map/reduce_scatter | solution.py:22
  1378.6 31.9 psum.236
  1434.8 30.9 convolution_bitcast_fusion.24
  1482.6 31.9 psum.237
  1552.0 40.6 %reduce-scatter.61.cloned.1.call-done = f32[1536,64]{0,1:T(8,128)} async-done(((f32[12288,64]{0,1:T(8,128)}), f32[1536,64]{0,1:T(8,128)}) %reduce-scatter.61.cloned.1.call-update) | async-done | bytes 393232 | tf_op jit(solution)/shard_map/reduce_scatter | solution.py:22
  1593.7 31.9 psum.238
  1649.9 30.9 convolution_bitcast_fusion.23
  1697.7 31.9 psum.239
  1766.9 40.6 %reduce-scatter.65.cloned.1.call-done = f32[1536,64]{0,1:T(8,128)} async-done(((f32[12288,64]{0,1:T(8,128)}), f32[1536,64]{0,1:T(8,128)}) %reduce-scatter.65.cloned.1.call-update) | async-done | bytes 393232 | tf_op jit(solution)/shard_map/reduce_scatter | solution.py:22
  1808.6 31.9 psum.240
  1864.8 30.9 convolution_bitcast_fusion.22
  1912.6 31.8 psum.241
  1981.8 40.6 %reduce-scatter.69.cloned.1.call-done = f32[1536,64]{0,1:T(8,128)} async-done(((f32[12288,64]{0,1:T(8,128)}), f32[1536,64]{0,1:T(8,128)}) %reduce-scatter.69.cloned.1.call-update) | async-done | bytes 393232 | tf_op jit(solution)/shard_map/reduce_scatter | solution.py:22
  2023.5 31.9 psum.242
  2079.7 30.9 convolution_bitcast_fusion.21
  2127.5 31.9 psum.243
  2196.7 40.6 %reduce-scatter.73.cloned.1.call-done = f32[1536,64]{0,1:T(8,128)} async-done(((f32[12288,64]{0,1:T(8,128)}), f32[1536,64]{0,1:T(8,128)}) %reduce-scatter.73.cloned.1.call-update) | async-done | bytes 393232 | tf_op jit(solution)/shard_map/reduce_scatter | solution.py:22
  2238.4 31.9 psum.244
  2294.6 30.9 convolution_bitcast_fusion.20
  2342.4 31.9 psum.245
  2411.9 40.6 %reduce-scatter.77.cloned.1.call-done = f32[1536,64]{0,1:T(8,128)} async-done(((f32[12288,64]{0,1:T(8,128)}), f32[1536,64]{0,1:T(8,128)}) %reduce-scatter.77.cloned.1.call-update) | async-done | bytes 393232 | tf_op jit(solution)/shard_map/reduce_scatter | solution.py:22
  2453.6 31.9 psum.246
  2509.8 30.9 convolution_bitcast_fusion.19
  2557.6 31.9 psum.247
  2626.7 40.6 %reduce-scatter.81.cloned.1.call-done = f32[1536,64]{0,1:T(8,128)} async-done(((f32[12288,64]{0,1:T(8,128)}), f32[1536,64]{0,1:T(8,128)}) %reduce-scatter.81.cloned.1.call-update) | async-done | bytes 393232 | tf_op jit(solution)/shard_map/reduce_scatter | solution.py:22
  2668.5 31.9 psum.248
  2724.7 30.9 convolution_bitcast_fusion.18
  2772.5 31.8 psum.249
  2841.6 40.6 %reduce-scatter.85.cloned.1.call-done = f32[1536,64]{0,1:T(8,128)} async-done(((f32[12288,64]{0,1:T(8,128)}), f32[1536,64]{0,1:T(8,128)}) %reduce-scatter.85.cloned.1.call-update) | async-done | bytes 393232 | tf_op jit(solution)/shard_map/reduce_scatter | solution.py:22
  2883.4 31.9 psum.250
  2939.6 30.9 convolution_bitcast_fusion.17
  2987.4 31.9 psum.251
  3056.6 40.6 %reduce-scatter.89.cloned.1.call-done = f32[1536,64]{0,1:T(8,128)} async-done(((f32[12288,64]{0,1:T(8,128)}), f32[1536,64]{0,1:T(8,128)}) %reduce-scatter.89.cloned.1.call-update) | async-done | bytes 393232 | tf_op jit(solution)/shard_map/reduce_scatter | solution.py:22
  3098.3 31.9 psum.252
  3154.5 30.9 convolution_bitcast_fusion.16
  3202.3 31.9 psum.253
  3271.6 40.6 %reduce-scatter.93.cloned.1.call-done = f32[1536,64]{0,1:T(8,128)} async-done(((f32[12288,64]{0,1:T(8,128)}), f32[1536,64]{0,1:T(8,128)}) %reduce-scatter.93.cloned.1.call-update) | async-done | bytes 393232 | tf_op jit(solution)/shard_map/reduce_scatter | solution.py:22
  3313.3 31.9 psum.254
  3369.7 30.9 convolution_bitcast_fusion.15
  3417.4 31.9 psum.255
  (311 shorter events, 1277.6 us)
Async XLA Ops:
  7.2 80.6 %reduce-scatter.33.cloned.1.call-start = ((), (), s32[]{:S(2)}) async-start(), calls=%async_computation.32 | async-start | bytes 3538944 | tf_op jit(solution)/shard_map/reduce_scatter | solution.py:22
  17.1 207.6 %copy-start = (f32[1536,64]{0,1:T(8,128)S(1)}, f32[1536,64]{0,1:T(8,128)}, u32[]{:S(2)}) copy-start(f32[1536,64]{0,1:T(8,128)} %param.4) | copy-start | bytes 1179652
  46.1 99.0 %all-gather.17.cloned.1.call-start = ((), (), s32[]{:S(2)}) async-start(), calls=%async_computation.33 | async-start | bytes 1769472 | tf_op jit(solution)/shard_map/all_gather | solution.py:24
  122.6 69.2 %reduce-scatter.35.cloned.1.call-start = ((), (), s32[]{:S(2)}) async-start(), calls=%async_computation.34 | async-start | bytes 1179648 | tf_op jit(solution)/shard_map/reduce_scatter | solution.py:26
  176.1 126.6 %reduce-scatter.37.cloned.1.call-start = ((), (), s32[]{:S(2)}) async-start(), calls=%async_computation.35 | async-start | bytes 3538944 | tf_op jit(solution)/shard_map/reduce_scatter | solution.py:22
  262.0 98.0 %all-gather.19.cloned.1.call-start = ((), (), s32[]{:S(2)}) async-start(), calls=%async_computation.36 | async-start | bytes 1769472 | tf_op jit(solution)/shard_map/all_gather | solution.py:24
  337.4 69.2 %reduce-scatter.39.cloned.1.call-start = ((), (), s32[]{:S(2)}) async-start(), calls=%async_computation.37 | async-start | bytes 1179648 | tf_op jit(solution)/shard_map/reduce_scatter | solution.py:26
  390.9 126.6 %reduce-scatter.41.cloned.1.call-start = ((), (), s32[]{:S(2)}) async-start(), calls=%async_computation.38 | async-start | bytes 3538944 | tf_op jit(solution)/shard_map/reduce_scatter | solution.py:22
  476.9 98.0 %all-gather.21.cloned.1.call-start = ((), (), s32[]{:S(2)}) async-start(), calls=%async_computation.39 | async-start | bytes 1769472 | tf_op jit(solution)/shard_map/all_gather | solution.py:24
  552.4 69.2 %reduce-scatter.43.cloned.1.call-start = ((), (), s32[]{:S(2)}) async-start(), calls=%async_computation.40 | async-start | bytes 1179648 | tf_op jit(solution)/shard_map/reduce_scatter | solution.py:26
  605.9 126.9 %reduce-scatter.45.cloned.1.call-start = ((), (), s32[]{:S(2)}) async-start(), calls=%async_computation.41 | async-start | bytes 3538944 | tf_op jit(solution)/shard_map/reduce_scatter | solution.py:22
  692.1 98.0 %all-gather.23.cloned.1.call-start = ((), (), s32[]{:S(2)}) async-start(), calls=%async_computation.42 | async-start | bytes 1769472 | tf_op jit(solution)/shard_map/all_gather | solution.py:24
  767.5 69.2 %reduce-scatter.47.cloned.1.call-start = ((), (), s32[]{:S(2)}) async-start(), calls=%async_computation.43 | async-start | bytes 1179648 | tf_op jit(solution)/shard_map/reduce_scatter | solution.py:26
  821.0 126.6 %reduce-scatter.49.cloned.1.call-start = ((), (), s32[]{:S(2)}) async-start(), calls=%async_computation.44 | async-start | bytes 3538944 | tf_op jit(solution)/shard_map/reduce_scatter | solution.py:22
  906.9 98.0 %all-gather.25.cloned.1.call-start = ((), (), s32[]{:S(2)}) async-start(), calls=%async_computation.45 | async-start | bytes 1769472 | tf_op jit(solution)/shard_map/all_gather | solution.py:24
  982.4 69.2 %reduce-scatter.51.cloned.1.call-start = ((), (), s32[]{:S(2)}) async-start(), calls=%async_computation.46 | async-start | bytes 1179648 | tf_op jit(solution)/shard_map/reduce_scatter | solution.py:26
  1035.9 126.6 %reduce-scatter.53.cloned.1.call-start = ((), (), s32[]{:S(2)}) async-start(), calls=%async_computation.47 | async-start | bytes 3538944 | tf_op jit(solution)/shard_map/reduce_scatter | solution.py:22
  1092.9 206.5 %copy-start.13 = (f32[64]{0:T(128)S(1)}, f32[64]{0:T(128)}, u32[]{:S(2)}) copy-start(f32[64]{0:T(128)} %get-tuple-element.14) | copy-start | bytes 772
  1092.9 206.5 %copy-start.24 = (f32[64]{0:T(128)S(1)}, f32[64]{0:T(128)}, u32[]{:S(2)}) copy-start(f32[64]{0:T(128)} %get-tuple-element.26) | copy-start | bytes 772
  1121.8 98.0 %all-gather.27.cloned.1.call-start = ((), (), s32[]{:S(2)}) async-start(), calls=%async_computation.48 | async-start | bytes 1769472 | tf_op jit(solution)/shard_map/all_gather | solution.py:24
  1197.3 69.2 %reduce-scatter.55.cloned.1.call-start = ((), (), s32[]{:S(2)}) async-start(), calls=%async_computation.49 | async-start | bytes 1179648 | tf_op jit(solution)/shard_map/reduce_scatter | solution.py:26
  1250.8 126.7 %reduce-scatter.57.cloned.1.call-start = ((), (), s32[]{:S(2)}) async-start(), calls=%async_computation.50 | async-start | bytes 3538944 | tf_op jit(solution)/shard_map/reduce_scatter | solution.py:22
  1307.9 206.5 %copy-start.12 = (f32[64]{0:T(128)S(1)}, f32[64]{0:T(128)}, u32[]{:S(2)}) copy-start(f32[64]{0:T(128)} %get-tuple-element.13) | copy-start | bytes 772
  1307.9 206.5 %copy-start.23 = (f32[64]{0:T(128)S(1)}, f32[64]{0:T(128)}, u32[]{:S(2)}) copy-start(f32[64]{0:T(128)} %get-tuple-element.27) | copy-start | bytes 772
  1336.8 98.0 %all-gather.29.cloned.1.call-start = ((), (), s32[]{:S(2)}) async-start(), calls=%async_computation.51 | async-start | bytes 1769472 | tf_op jit(solution)/shard_map/all_gather | solution.py:24
  1412.2 69.2 %reduce-scatter.59.cloned.1.call-start = ((), (), s32[]{:S(2)}) async-start(), calls=%async_computation.52 | async-start | bytes 1179648 | tf_op jit(solution)/shard_map/reduce_scatter | solution.py:26
  1465.7 126.9 %reduce-scatter.61.cloned.1.call-start = ((), (), s32[]{:S(2)}) async-start(), calls=%async_computation.53 | async-start | bytes 3538944 | tf_op jit(solution)/shard_map/reduce_scatter | solution.py:22
  1523.0 206.5 %copy-start.11 = (f32[64]{0:T(128)S(1)}, f32[64]{0:T(128)}, u32[]{:S(2)}) copy-start(f32[64]{0:T(128)} %get-tuple-element.12) | copy-start | bytes 772
  1523.0 206.5 %copy-start.22 = (f32[64]{0:T(128)S(1)}, f32[64]{0:T(128)}, u32[]{:S(2)}) copy-start(f32[64]{0:T(128)} %get-tuple-element.28) | copy-start | bytes 772
  1551.9 98.0 %all-gather.31.cloned.1.call-start = ((), (), s32[]{:S(2)}) async-start(), calls=%async_computation.54 | async-start | bytes 1769472 | tf_op jit(solution)/shard_map/all_gather | solution.py:24
  1627.4 69.2 %reduce-scatter.63.cloned.1.call-start = ((), (), s32[]{:S(2)}) async-start(), calls=%async_computation.55 | async-start | bytes 1179648 | tf_op jit(solution)/shard_map/reduce_scatter | solution.py:26
  1680.9 126.6 %reduce-scatter.65.cloned.1.call-start = ((), (), s32[]{:S(2)}) async-start(), calls=%async_computation.56 | async-start | bytes 3538944 | tf_op jit(solution)/shard_map/reduce_scatter | solution.py:22
  1766.8 98.0 %all-gather.33.cloned.1.call-start = ((), (), s32[]{:S(2)}) async-start(), calls=%async_computation.57 | async-start | bytes 1769472 | tf_op jit(solution)/shard_map/all_gather | solution.py:24
  1842.3 69.2 %reduce-scatter.67.cloned.1.call-start = ((), (), s32[]{:S(2)}) async-start(), calls=%async_computation.58 | async-start | bytes 1179648 | tf_op jit(solution)/shard_map/reduce_scatter | solution.py:26
  1895.8 126.6 %reduce-scatter.69.cloned.1.call-start = ((), (), s32[]{:S(2)}) async-start(), calls=%async_computation.59 | async-start | bytes 3538944 | tf_op jit(solution)/shard_map/reduce_scatter | solution.py:22
  1952.8 206.5 %copy-start.20 = (f32[64]{0:T(128)S(1)}, f32[64]{0:T(128)}, u32[]{:S(2)}) copy-start(f32[64]{0:T(128)} %get-tuple-element.30) | copy-start | bytes 772
  1981.7 98.0 %all-gather.35.cloned.1.call-start = ((), (), s32[]{:S(2)}) async-start(), calls=%async_computation.60 | async-start | bytes 1769472 | tf_op jit(solution)/shard_map/all_gather | solution.py:24
  2057.2 69.2 %reduce-scatter.71.cloned.1.call-start = ((), (), s32[]{:S(2)}) async-start(), calls=%async_computation.61 | async-start | bytes 1179648 | tf_op jit(solution)/shard_map/reduce_scatter | solution.py:26
  2110.7 126.7 %reduce-scatter.73.cloned.1.call-start = ((), (), s32[]{:S(2)}) async-start(), calls=%async_computation.62 | async-start | bytes 3538944 | tf_op jit(solution)/shard_map/reduce_scatter | solution.py:22
  2167.8 206.5 %copy-start.8 = (f32[64]{0:T(128)S(1)}, f32[64]{0:T(128)}, u32[]{:S(2)}) copy-start(f32[64]{0:T(128)} %get-tuple-element.9) | copy-start | bytes 772
  2167.8 206.5 %copy-start.19 = (f32[64]{0:T(128)S(1)}, f32[64]{0:T(128)}, u32[]{:S(2)}) copy-start(f32[64]{0:T(128)} %get-tuple-element.31) | copy-start | bytes 772
  2196.7 98.0 %all-gather.37.cloned.1.call-start = ((), (), s32[]{:S(2)}) async-start(), calls=%async_computation.63 | async-start | bytes 1769472 | tf_op jit(solution)/shard_map/all_gather | solution.py:24
  2272.1 69.2 %reduce-scatter.75.cloned.1.call-start = ((), (), s32[]{:S(2)}) async-start(), calls=%async_computation.64 | async-start | bytes 1179648 | tf_op jit(solution)/shard_map/reduce_scatter | solution.py:26
  2325.6 126.9 %reduce-scatter.77.cloned.1.call-start = ((), (), s32[]{:S(2)}) async-start(), calls=%async_computation.65 | async-start | bytes 3538944 | tf_op jit(solution)/shard_map/reduce_scatter | solution.py:22
  2382.9 206.5 %copy-start.18 = (f32[64]{0:T(128)S(1)}, f32[64]{0:T(128)}, u32[]{:S(2)}) copy-start(f32[64]{0:T(128)} %get-tuple-element.32) | copy-start | bytes 772
  2411.8 98.0 %all-gather.39.cloned.1.call-start = ((), (), s32[]{:S(2)}) async-start(), calls=%async_computation.66 | async-start | bytes 1769472 | tf_op jit(solution)/shard_map/all_gather | solution.py:24
  2487.3 69.2 %reduce-scatter.79.cloned.1.call-start = ((), (), s32[]{:S(2)}) async-start(), calls=%async_computation.67 | async-start | bytes 1179648 | tf_op jit(solution)/shard_map/reduce_scatter | solution.py:26
  2540.8 126.6 %reduce-scatter.81.cloned.1.call-start = ((), (), s32[]{:S(2)}) async-start(), calls=%async_computation.68 | async-start | bytes 3538944 | tf_op jit(solution)/shard_map/reduce_scatter | solution.py:22
  2626.7 98.0 %all-gather.41.cloned.1.call-start = ((), (), s32[]{:S(2)}) async-start(), calls=%async_computation.69 | async-start | bytes 1769472 | tf_op jit(solution)/shard_map/all_gather | solution.py:24
  2702.1 69.2 %reduce-scatter.83.cloned.1.call-start = ((), (), s32[]{:S(2)}) async-start(), calls=%async_computation.70 | async-start | bytes 1179648 | tf_op jit(solution)/shard_map/reduce_scatter | solution.py:26
  2755.6 126.6 %reduce-scatter.85.cloned.1.call-start = ((), (), s32[]{:S(2)}) async-start(), calls=%async_computation.71 | async-start | bytes 3538944 | tf_op jit(solution)/shard_map/reduce_scatter | solution.py:22
  2812.7 206.5 %copy-start.16 = (f32[64]{0:T(128)S(1)}, f32[64]{0:T(128)}, u32[]{:S(2)}) copy-start(f32[64]{0:T(128)} %get-tuple-element.34) | copy-start | bytes 772
  2841.6 98.0 %all-gather.43.cloned.1.call-start = ((), (), s32[]{:S(2)}) async-start(), calls=%async_computation.72 | async-start | bytes 1769472 | tf_op jit(solution)/shard_map/all_gather | solution.py:24
  2917.0 69.2 %reduce-scatter.87.cloned.1.call-start = ((), (), s32[]{:S(2)}) async-start(), calls=%async_computation.73 | async-start | bytes 1179648 | tf_op jit(solution)/shard_map/reduce_scatter | solution.py:26
  2970.5 126.7 %reduce-scatter.89.cloned.1.call-start = ((), (), s32[]{:S(2)}) async-start(), calls=%async_computation.74 | async-start | bytes 3538944 | tf_op jit(solution)/shard_map/reduce_scatter | solution.py:22
  3027.6 206.5 %copy-start.4 = (f32[64]{0:T(128)S(1)}, f32[64]{0:T(128)}, u32[]{:S(2)}) copy-start(f32[64]{0:T(128)} %get-tuple-element.5) | copy-start | bytes 772
  3027.6 206.5 %copy-start.15 = (f32[64]{0:T(128)S(1)}, f32[64]{0:T(128)}, u32[]{:S(2)}) copy-start(f32[64]{0:T(128)} %get-tuple-element.23) | copy-start | bytes 772
  3056.5 98.0 %all-gather.45.cloned.1.call-start = ((), (), s32[]{:S(2)}) async-start(), calls=%async_computation.75 | async-start | bytes 1769472 | tf_op jit(solution)/shard_map/all_gather | solution.py:24
  3132.0 69.2 %reduce-scatter.91.cloned.1.call-start = ((), (), s32[]{:S(2)}) async-start(), calls=%async_computation.76 | async-start | bytes 1179648 | tf_op jit(solution)/shard_map/reduce_scatter | solution.py:26
  3185.5 126.7 %reduce-scatter.93.cloned.1.call-start = ((), (), s32[]{:S(2)}) async-start(), calls=%async_computation.77 | async-start | bytes 3538944 | tf_op jit(solution)/shard_map/reduce_scatter | solution.py:22
  3242.6 206.7 %copy-start.2 = (f32[64]{0:T(128)S(1)}, f32[64]{0:T(128)}, u32[]{:S(2)}) copy-start(f32[64]{0:T(128)} %get-tuple-element.4) | copy-start | bytes 772
  3242.6 206.7 %copy-start.3 = (f32[64]{0:T(128)S(1)}, f32[64]{0:T(128)}, u32[]{:S(2)}) copy-start(f32[64]{0:T(128)} %get-tuple-element.20) | copy-start | bytes 772
  3271.5 98.1 %all-gather.47.cloned.1.call-start = ((), (), s32[]{:S(2)}) async-start(), calls=%async_computation.78 | async-start | bytes 1769472 | tf_op jit(solution)/shard_map/all_gather | solution.py:24
  3347.1 69.2 %reduce-scatter.95.cloned.1.call-start = ((), (), s32[]{:S(2)}) async-start(), calls=%async_computation.79 | async-start | bytes 1179648 | tf_op jit(solution)/shard_map/reduce_scatter | solution.py:26
  (10 other events, 2017.8 us)
Sparse Core Ops, SparseCore 0:
  46.3 41.4 reduce-scatter.32
  122.7 22.3 all-gather.16
  176.2 15.5 reduce-scatter.34
  262.1 40.5 reduce-scatter.36
  337.6 22.3 all-gather.18
  391.1 15.5 reduce-scatter.38
  477.0 40.5 reduce-scatter.40
  552.5 22.3 all-gather.20
  606.0 15.5 reduce-scatter.42
  692.2 40.5 reduce-scatter.44
  767.6 22.3 all-gather.22
  821.1 15.5 reduce-scatter.46
  907.1 40.5 reduce-scatter.48
  982.5 22.3 all-gather.24
  1036.0 15.5 reduce-scatter.50
  1122.0 40.5 reduce-scatter.52
  1197.4 22.3 all-gather.26
  1250.9 15.5 reduce-scatter.54
  1336.9 40.5 reduce-scatter.56
  1412.4 22.3 all-gather.28
  1465.9 15.5 reduce-scatter.58
  1552.1 40.5 reduce-scatter.60
  1627.5 22.3 all-gather.30
  1681.0 15.5 reduce-scatter.62
  1766.9 40.5 reduce-scatter.64
  1842.4 22.3 all-gather.32
  1895.9 15.5 reduce-scatter.66
  1981.8 40.5 reduce-scatter.68
  2057.3 22.3 all-gather.34
  2110.8 15.5 reduce-scatter.70
  2196.8 40.5 reduce-scatter.72
  2272.2 22.3 all-gather.36
  2325.7 15.5 reduce-scatter.74
  2411.9 40.5 reduce-scatter.76
  2487.4 22.3 all-gather.38
  2540.9 15.5 reduce-scatter.78
  2626.8 40.5 reduce-scatter.80
  2702.3 22.3 all-gather.40
  2755.8 15.5 reduce-scatter.82
  2841.7 40.5 reduce-scatter.84
  2917.2 22.3 all-gather.42
  2970.7 15.5 reduce-scatter.86
  3056.7 40.5 reduce-scatter.88
  3132.1 22.3 all-gather.44
  3185.6 15.5 reduce-scatter.90
  3271.6 40.5 reduce-scatter.92
  3347.2 22.3 all-gather.46
  3400.7 15.5 reduce-scatter.94
where the time goes:
time: 3470 us; the launch traced here: 3460 us
  waiting for transfers between devices  1260 us (36%)
  blocking collectives  1140 us (33%)
  matrix products  957 us (28%)
  other arithmetic  85.5 us (2%)
    psum x32, blocking collectives, col_normalise(): lax.psum(jnp.sum(local_vals * local_vals, axis=0, keepdims=True), ('col',...  1020 us
    reduce_scatter x16, waiting for transfers between devices, device_fn(): lax.psum_scatter(auth_part, 'row', scatter_dimension=0, tiled=True)  651 us
    dot_general x16, matrix products, device_fn(): hub_part = jnp.dot(adj_tile, auth_block, preferred_element_type=jnp.float32)  495 us
    dot_general x16, matrix products, device_fn(): lax.dot_general(adj_tile, hub_block, (((0,), (0,)), ((), ())), preferred_...  462 us
    all_gather x16, waiting for transfers between devices, device_fn(): lax.all_gather(auth_vec.astype(jnp.bfloat16), 'row', axis=0, tiled=True)  360 us
    reduce_scatter x16, waiting for transfers between devices, device_fn(): hub_sum = lax.psum_scatter(hub_part, 'col', scatter_dimension=0, tiled=True)  249 us
    all_gather x16, blocking collectives, device_fn(): lax.all_gather(hub_vec.astype(jnp.bfloat16), 'col', axis=0, tiled=True)  118 us
  transfers between devices with their start and end apart: 48, of which 48 were waited for; matrix products, arithmetic and copies ran while one was open for 0% of the time, Pallas kernels for 0%

commit v1 on v0

v1 whole, which is shorter than its diff:
```python
import functools

import jax
import jax.numpy as jnp
from jax import lax
from jax.experimental import pallas as pl
from jax.experimental.pallas import tpu as pltpu
from jax.sharding import PartitionSpec as P

F32, BF16 = jnp.float32, jnp.bfloat16
MESH = pl.DeviceIdType.MESH
SLOTS = 6


def prod_cols(lhs, rhs):
    return lax.dot_general(lhs, rhs, (((1,), (0,)), ((), ())), preferred_element_type=F32)


def prod_rows(lhs, rhs):
    return lax.dot_general(lhs, rhs, (((1,), (1,)), ((), ())), preferred_element_type=F32)


def lane_tile(v, width):
    return jnp.concatenate([v] * (width // 128), axis=1)


def square_sums(parts):
    total = None
    for part in parts:
        for t in range(part.shape[1] // 128):
            v = part[:, t * 128:(t + 1) * 128]
            total = v * v if total is None else total + v * v
    full = jnp.concatenate([total, jnp.zeros((128 - total.shape[0], 128), F32)], axis=0)
    row = jnp.sum(full.T, axis=0, keepdims=True)
    return jnp.broadcast_to(row, (8, 128))


def kernel(n_total, v_ref, b_ref, a_hbm, auth_out, hub_out,
           res, stm, hb, ab, acc, hub, rd, s1x, s1y, s2x, s2y, zr, sq_send, sq1, sq2,
           res_sem, stm_sem, dd_s, dd_r, x1_s, x1_r, y1_s, y1_r, x2_s, x2_r, y2_s, y2_r,
           ag_s, ag_r, z_s, z_r, h_s, h_r, q1_s, q1_r, q2_s, q2_r):
    sweeps, dim = b_ref.shape[0], v_ref.shape[0]
    rows, width = stm.shape[1], stm.shape[2]
    j, i = lax.axis_index("col"), lax.axis_index("row")
    core, x, y = i % 2, (i // 2) % 2, i // 4
    partner = {"row": i + 1 - 2 * core, "col": j}
    xnb = {"row": i + 2 - 4 * x, "col": j}
    ynb = {"row": i + 4 - 8 * y, "col": j}
    znb = {"row": i, "col": 1 - j}
    base_o, base_x = 4 * y + 2 * x, 4 * y + 2 * (1 - x)
    base_y, base_d = 4 * (1 - y) + 2 * x, 4 * (1 - y) + 2 * (1 - x)
    mine, other = core, 1 - core
    ord1 = [base_d + other, base_d + mine, base_x + other, base_x + mine,
            base_y + other, base_y + mine, base_o + other, base_o + mine]
    ord2 = [base_o + other, base_o + mine, base_x + mine, base_y + mine,
            base_x + other, base_y + other, base_d + other, base_d + mine]

    def rcopy(src, dst, s, r, dev):
        return pltpu.make_async_remote_copy(src, dst, s, r, device_id=dev, device_id_type=MESH)

    def a_block(which, chunk, half):
        return a_hbm.at[pl.ds(pl.multiple_of(which * rows, rows), rows),
                        pl.ds(pl.multiple_of((chunk * 2 + half) * width, width), width)]

    def load(chunk, half, slot):
        return pltpu.make_async_copy(a_block(1 - j, chunk, half), stm.at[slot], stm_sem.at[slot])

    def load_res(u):
        return pltpu.make_async_copy(a_block(j, u // 2, u % 2), res.at[u // 2, u % 2], res_sem.at[u])

    def stream_unit(ci, half, order, after):
        slot = (2 * ci + half) % SLOTS
        if ci >= 2:
            load(order[ci], half, slot).wait()

        def done():
            if ci <= 4:
                load(order[ci + 3], half, slot).start()
            elif ci == 5:
                load(after[2], half, slot).start()
        return slot, done

    def copies_h():
        return rcopy(hb.at[0], hb.at[1], h_s, h_r, znb)

    def all_sum(row8, buf, send, recv):
        sq_send[...] = row8
        buf[0] = row8
        copies = []
        for d in range(15, 0, -1):
            dz, dy, dx, dc = d // 8, (d // 4) % 2, (d // 2) % 2, d % 2
            dev = {"row": 4 * ((y + dy) % 2) + 2 * ((x + dx) % 2) + (core + dc) % 2, "col": (j + dz) % 2}
            copies.append(rcopy(sq_send, buf.at[d], send.at[d], recv.at[d], dev))
            copies[-1].start()
        for c in copies:
            c.wait_recv()
        vals = [buf[d] for d in range(16)]
        while len(vals) > 1:
            vals = [vals[q] + vals[q + 1] for q in range(0, len(vals), 2)]
        scale = lax.rsqrt(vals[0] / n_total)
        cols = jnp.concatenate([scale] * 16, axis=0).T[:dim]
        for c in copies:
            c.wait_send()
        return cols

    for u in range(16):
        load_res(u).start()
    for u in range(SLOTS):
        load(ord1[u // 2], u % 2, u).start()
    hb[0] = v_ref[...].astype(BF16)
    copies_h().start()
    for u in range(16):
        load_res(u).wait()
    for u in range(4):
        load(ord1[u // 2], u % 2, u).wait()

    def sweep(k, carry):
        def own(u, c):
            acc[u // 2, u % 2] = prod_cols(hb[0], res[u // 2, u % 2])
            return c
        lax.fori_loop(0, 16, own, 0)
        h_cp = copies_h()
        h_cp.wait_recv()

        dd = [rcopy(acc.at[ord1[2 * t]], rd.at[t], dd_s.at[t], dd_r.at[t], partner) for t in range(4)]
        d_mine, x_mine, y_mine, o_mine = ord1[1], ord1[3], ord1[5], ord1[7]
        x1 = [rcopy(acc.at[d_mine, 0], s1x.at[0], x1_s.at[0], x1_r.at[0], xnb),
              rcopy(acc.at[x_mine, 0], s1x.at[1], x1_s.at[1], x1_r.at[1], xnb)]
        y1 = [rcopy(acc.at[d_mine, 1], s1y.at[0], y1_s.at[0], y1_r.at[0], ynb),
              rcopy(acc.at[y_mine, 1], s1y.at[1], y1_s.at[1], y1_r.at[1], ynb)]
        x2 = rcopy(acc.at[x_mine, 1], s2x, x2_s, x2_r, xnb)
        y2 = rcopy(acc.at[y_mine, 0], s2y, y2_s, y2_r, ynb)

        def other_rows(ci):
            chunk = ord1[ci]

            def unit(half, c):
                slot, done = stream_unit(ci, half, ord1, ord2)
                acc[chunk, half] += prod_cols(hb[1], stm[slot])
                done()
                return c
            lax.fori_loop(0, 2, unit, 0)

        def combine(t):
            dd[t].wait_recv()
            m = ord1[2 * t + 1]
            acc[m] += rd[t]

        other_rows(0)
        dd[0].start()
        other_rows(1)
        other_rows(2)
        dd[1].start()
        combine(0)
        x1[0].start()
        y1[0].start()
        other_rows(3)
        other_rows(4)
        dd[2].start()
        combine(1)
        x1[1].start()
        other_rows(5)
        other_rows(6)
        dd[3].start()
        combine(2)
        y1[1].start()
        other_rows(7)
        x1[0].wait_recv()
        acc[y_mine, 0] += s1x[0]
        y2.start()
        y1[0].wait_recv()
        acc[x_mine, 1] += s1y[0]
        x2.start()
        combine(3)
        x1[1].wait_recv()
        y1[1].wait_recv()
        p0 = acc[o_mine, 0] + s1x[1]
        p1 = acc[o_mine, 1] + s1y[1]
        acc[o_mine, 0] = p0
        acc[o_mine, 1] = p1
        y2.wait_recv()
        x2.wait_recv()
        p0 = acc[o_mine, 0] + s2y[...]
        p1 = acc[o_mine, 1] + s2x[...]
        auth_out[0] = p0
        auth_out[1] = p1
        scale = all_sum(square_sums([p0, p1]), sq1, q1_s, q1_r)
        wide = lane_tile(scale, width)
        for half in range(2):
            val = auth_out[half] * wide
            auth_out[half] = val
            ab[i, half] = val.astype(BF16)
        for c in dd + x1 + y1 + [x2, y2, h_cp]:
            c.wait_send()

        px, py, pd = ord1[3], ord1[5], ord1[1]
        to_p = rcopy(ab.at[i], ab.at[i], ag_s.at[0], ag_r.at[0], partner)
        to_x = [rcopy(ab.at[i, h], ab.at[i, h], ag_s.at[1 + h], ag_r.at[1 + h], xnb) for h in range(2)]
        to_y = [rcopy(ab.at[i, h], ab.at[i, h], ag_s.at[3 + h], ag_r.at[3 + h], ynb) for h in range(2)]
        rel_y = rcopy(ab.at[px, 0], ab.at[px, 0], ag_s.at[5], ag_r.at[5], ynb)
        rel_x = rcopy(ab.at[py, 1], ab.at[py, 1], ag_s.at[6], ag_r.at[6], xnb)
        fw_x = rcopy(ab.at[px], ab.at[px], ag_s.at[7], ag_r.at[7], partner)
        fw_y = rcopy(ab.at[py], ab.at[py], ag_s.at[8], ag_r.at[8], partner)
        fw_d = rcopy(ab.at[pd], ab.at[pd], ag_s.at[9], ag_r.at[9], partner)
        to_p.start()
        to_x[0].start()
        to_y[1].start()
        to_x[1].start()
        to_y[0].start()

        def resident(chunk, first):
            def unit(half, c):
                val = prod_rows(ab[chunk, half], res[chunk, half])
                if first:
                    @pl.when(half == 0)
                    def _():
                        hub[0] = val

                    @pl.when(half != 0)
                    def _():
                        hub[0] += val
                else:
                    hub[0] += val
                return c
            lax.fori_loop(0, 2, unit, 0)

        def streamed(ci):
            chunk = ord2[ci]

            def unit(half, c):
                slot, done = stream_unit(ci, half, ord2, ord1)
                hub[1] += prod_rows(ab[chunk, half], stm[slot])
                done()
                return c
            lax.fori_loop(0, 2, unit, 0)

        hub[0] = jnp.zeros(hub.shape[1:], F32)
        hub[1] = jnp.zeros(hub.shape[1:], F32)
        resident(ord2[1], False)
        streamed(1)
        to_p.wait_recv()
        resident(ord2[0], False)
        streamed(0)
        to_x[0].wait_recv()
        rel_y.start()
        to_y[1].wait_recv()
        rel_x.start()
        to_x[1].wait_recv()
        fw_x.start()
        to_y[0].wait_recv()
        fw_y.start()
        streamed(2)
        streamed(3)
        fw_x.wait_recv()
        streamed(4)
        rel_y.wait_recv()
        rel_x.wait_recv()
        fw_d.start()
        fw_y.wait_recv()
        streamed(5)
        fw_d.wait_recv()
        streamed(6)
        streamed(7)
        z_cp = rcopy(hub.at[1], zr, z_s, z_r, znb)
        z_cp.start()

        def rest(u, c):
            chunk = (base_o + 2 + u // 2) % 8
            half = u % 2
            hub[0] += prod_rows(ab[chunk, half], res[chunk, half])
            return c
        lax.fori_loop(0, 12, rest, 0)
        z_cp.wait_recv()
        val = hub[0] + zr[...]
        hub[0] = val
        scale = all_sum(square_sums([val]), sq2, q2_s, q2_r)
        wt = b_ref[k]
        keep = lane_tile((1.0 - wt) * 1.0, 2 * width)
        hv = keep * (hub[0] * lane_tile(scale, 2 * width)) + lane_tile(wt, 2 * width) * v_ref[...]
        hub_out[...] = hv
        hb[0] = hv.astype(BF16)
        for c in [to_p, *to_x, *to_y, rel_y, rel_x, fw_x, fw_y, fw_d, z_cp]:
            c.wait_send()

        @pl.when(k < sweeps - 1)
        def _():
            copies_h().start()
        return carry

    lax.fori_loop(0, sweeps, sweep, 0)
    for half in range(2):
        load(ord1[2], half, 4 + half).wait()


def solution(mesh):
    def device_fn(adj_tile, pers_piece, restart_wt):
        sweeps, dim = restart_wt.shape
        chunk = pers_piece.shape[0]
        width = chunk // 2
        n_total = float(chunk * mesh.size)
        wt = jnp.broadcast_to(restart_wt[:, :, None], (sweeps, dim, 128))
        vmem = pl.BlockSpec(memory_space=pltpu.VMEM)
        dma = pltpu.SemaphoreType.DMA
        auth, hub = pl.pallas_call(
            functools.partial(kernel, n_total),
            out_shape=(jax.ShapeDtypeStruct((2, dim, width), F32), jax.ShapeDtypeStruct((dim, chunk), F32)),
            in_specs=[vmem, vmem, pl.BlockSpec(memory_space=pl.ANY)],
            out_specs=(vmem, vmem),
            scratch_shapes=[
                pltpu.VMEM((8, 2, chunk, width), BF16),
                pltpu.VMEM((SLOTS, chunk, width), BF16),
                pltpu.VMEM((2, dim, chunk), BF16),
                pltpu.VMEM((8, 2, dim, width), BF16),
                pltpu.VMEM((8, 2, dim, width), F32),
                pltpu.VMEM((2, dim, chunk), F32),
                pltpu.VMEM((4, 2, dim, width), F32),
                pltpu.VMEM((2, dim, width), F32),
                pltpu.VMEM((2, dim, width), F32),
                pltpu.VMEM((dim, width), F32),
                pltpu.VMEM((dim, width), F32),
                pltpu.VMEM((dim, chunk), F32),
                pltpu.VMEM((8, 128), F32),
                pltpu.VMEM((16, 8, 128), F32),
                pltpu.VMEM((16, 8, 128), F32),
                dma((16,)), dma((SLOTS,)), dma((4,)), dma((4,)), dma((2,)), dma((2,)), dma((2,)), dma((2,)),
                dma, dma, dma, dma, dma((10,)), dma((10,)), dma, dma, dma, dma,
                dma((16,)), dma((16,)), dma((16,)), dma((16,)),
            ],
            compiler_params=pltpu.CompilerParams(vmem_limit_bytes=67043328, has_side_effects=True),
        )(pers_piece.T, wt, adj_tile)
        return auth.transpose(0, 2, 1).reshape(chunk, dim), hub.T

    return jax.shard_map(
        device_fn, mesh=mesh,
        in_specs=(P("row", "col"), P(("row", "col"), None), P(None, None)),
        out_specs=(P(("col", "row"), None), P(("row", "col"), None)), check_vma=False)
```

time: 3470 us -> 1010 us (0.29)
  waiting for transfers between devices: 1260 us -> 0 us
  blocking collectives: 1140 us -> 0 us
  Pallas kernels: 0 us -> 1000 us
  matrix products: 957 us -> 0 us
  other arithmetic: 85.5 us -> 0 us
    psum x32 -> x0, blocking collectives: 1020 us -> none  [col_normalise(): lax.psum(jnp.sum(local_vals * local_vals, axis=0, keepdims=True), ('col',...]
    pallas_call x0 -> x1, Pallas kernels: none -> 1000 us  [device_fn(): pl.pallas_call(functools.partial(kernel, n_total), out_shape=(jax.ShapeDt...]
    dot_general x32 -> x0, matrix products: 957 us -> none  [the longest x16 495 us: device_fn(): hub_part = jnp.dot(adj_tile, auth_block, preferred_element_type=jnp.float32)]
    reduce_scatter x32 -> x0, waiting for transfers between devices: 900 us -> none  [the longest x16 651 us: device_fn(): lax.psum_scatter(auth_part, 'row', scatter_dimension=0, tiled=True)]
    all_gather x16 -> x0, waiting for transfers between devices: 360 us -> none  [device_fn(): lax.all_gather(auth_vec.astype(jnp.bfloat16), 'row', axis=0, tiled=True)]
    all_gather x16 -> x0, blocking collectives: 118 us -> none  [device_fn(): lax.all_gather(hub_vec.astype(jnp.bfloat16), 'col', axis=0, tiled=True)]
    convert_element_type x32 -> x0, other arithmetic: 46.3 us -> none  [the longest x16 28.4 us: device_fn(): auth_vec.astype(jnp.bfloat16)]
    reduce_sum x32 -> x0, other arithmetic: 35.9 us -> none  [col_normalise(): jnp.sum(local_vals * local_vals, axis=0, keepdims=True)]
  transfers between devices with their start and end apart: 48 -> 0, of which waited for: 48 -> 0; matrix products, arithmetic and copies ran while one was open for 0% -> 0% of each run, Pallas kernels for 0% -> 0%
where the time goes in v1:
time: 1010 us
  Pallas kernels  1000 us (99%)
    pallas_call x1, Pallas kernels, device_fn(): pl.pallas_call(functools.partial(kernel, n_total), out_shape=(jax.ShapeDt...  1000 us

profile of v1, /device:TPU:0, one launch (start us, length us, event | category | flops | bytes accessed | tf_op | source)
XLA Modules:
  0.0 1008.3 jit_solution(17528386202483827801)
XLA Ops:
  0.6 1.7 broadcast_in_dim.2.b_ref
  2.3 1002.4 %shard_map.50 = (f32[2,64,768]{2,1,0:T(8,128)}, f32[64,1536]{1,0:T(8,128)}) custom-call(f32[64,1536]{1,0:T(8,128)} %bitcast.5, f32[16,64,128]{2,1,0:T(8,128)} %broadcast_in_dim.2.b_ref, bf16[3072,12288]{1,0:T(8,128)(2,1)} %a_hbm.1), custom_call_target="tpu_custom_call" | custom-call | tf_op jit(solution)/shard_map/pallas_call | solution.py:304
  1004.7 1.8 copy.6
  1006.5 1.8 copy.8
